TPU v7x, 512 devices: a whole 4x8x8 slice. The times are simulated.
512 devices in a mesh: dp: 16 (over x, y_lo, core), pipe: 8 (over z), tensor: 4 (over y_hi).
Axes of the slice: x: 4, y: 8 (y_hi: 4, y_lo: 2; y = y_hi * 2 + y_lo), z: 8, core: 2. Of those that a mesh axis runs over, the one named last changes fastest.
Arguments:
- weights: bfloat16 [11264, 1408], P(('dp', 'pipe', 'tensor')), may hold values from -6 to 6
- first_moment: bfloat16 [11264, 1408], P(('dp', 'pipe', 'tensor')), may hold values from -6 to 6
- second_moment: bfloat16 [11264, 1408], P(('dp', 'pipe', 'tensor')), may hold values from 0.049804688 to 5
- row_weight: float32 [1408], replicated, may hold values from -1 to 1
- col_weight: float32 [1408], replicated, may hold values from 1 to 4
Outputs:
- weight_tiles: bfloat16 [11264, 1408], P(('pipe', 'tensor'))
- first_tiles: bfloat16 [11264, 1408], P(('pipe', 'tensor'))
- second_tiles: bfloat16 [11264, 1408], P(('pipe', 'tensor'))
- checksums: float32 [3, 8, 4, 11], P(None, 'pipe', 'tensor')
All inputs are finite; a program needn't handle non-finite values.
Results may differ from a plain program's by a relative error of at most 0.001.
Values may be sent and summed in bfloat16 or wider, within the bound.
A program may use at most 64 MiB of HBM per device.

v0:
```python
import jax
import jax.numpy as jnp
from jax import lax
from jax.sharding import Mesh
from jax.sharding import PartitionSpec as P

CHECK_COLS = 128
DP = ("dp_0", "dp_1", "dp_2")
DP_PIPE_TENSOR = ("dp_0", "dp_1", "dp_2", "pipe", "tensor")


def for_sending(array):
    return jax.tree.map(lambda a: a.astype(jnp.bfloat16) if a.dtype == jnp.float32 else a, array)


def laid_out(blocks, dim):
    dims = list(blocks.shape[1:])
    dims[dim] *= blocks.shape[0]
    return jnp.moveaxis(blocks, 0, dim).reshape(dims)


def gather_in_order(array, axes, order):
    blocks = array[None]
    for k in order:
        blocks = lax.all_gather(blocks, axes[k], axis=0, tiled=True)
    block = [lax.axis_size(axes[k]) for k in reversed(order)]
    blocks = blocks.reshape(*block, *array.shape)
    turned = sorted(range(len(order)), key=lambda place: order[len(order) - 1 - place])
    return blocks.transpose(*turned, *range(len(order), blocks.ndim)).reshape(-1, *array.shape)


def gather_axes(array, axes, order, dim):
    return laid_out(gather_in_order(array, axes, order), dim)


def column_sums(data, row_part, col_weight, col_blocks):
    row_mixed = jnp.dot(
        row_part[None, :], data.astype(jnp.float32), precision=lax.Precision.HIGHEST
    )[0]
    return jnp.sum((row_mixed * col_weight).reshape(col_blocks, -1), axis=1)


def shards(weights, first_moment, second_moment, row_weight, col_weight):
    dp_count = lax.axis_size(DP)
    pipe_count = lax.axis_size("pipe")
    tensor_count = lax.axis_size("tensor")
    shard_rows, width = weights.shape
    dp_section = dp_count // pipe_count
    tile_shards = dp_count // tensor_count
    piece_cols = width // dp_count
    tile_rows = shard_rows * dp_count
    col_blocks = width // CHECK_COLS
    factor = float(tile_rows * CHECK_COLS) ** (-0.5)
    sources = (weights, first_moment, second_moment)
    exchanged = (
        lax.all_to_all(sources[0], DP, split_axis=1, concat_axis=0, tiled=True),
        lax.all_to_all(sources[1], DP, split_axis=1, concat_axis=0, tiled=True),
        lax.all_to_all(sources[2], DP, split_axis=1, concat_axis=0, tiled=True),
    )
    grouped = tuple(
        (item.reshape(pipe_count, dp_section, shard_rows, piece_cols) for item in exchanged)
    )
    sectioned = jax.tree.map(
        lambda part, own: part.astype(own.dtype),
        lax.all_to_all(for_sending(grouped), "pipe", split_axis=0, concat_axis=2, tiled=True),
        grouped,
    )
    routed = tuple(
        (item.reshape(tensor_count, tile_shards, 1, shard_rows, piece_cols) for item in sectioned)
    )
    arrived = jax.tree.map(
        lambda part, own: part.astype(own.dtype),
        lax.all_to_all(for_sending(routed), "tensor", split_axis=0, concat_axis=2, tiled=True),
        routed,
    )
    flat_pieces = tuple((item.reshape(tile_rows, piece_cols) for item in arrived))
    tiles = jax.tree.map(
        lambda part, own: part.astype(own.dtype),
        jax.tree.map(lambda part: gather_axes(part, DP, (1, 0, 2), 1), for_sending(flat_pieces)),
        flat_pieces,
    )
    tensor_pos = lax.axis_index("tensor")
    row_part = lax.dynamic_slice_in_dim(row_weight, tensor_pos * tile_rows, tile_rows)
    local_sums = jnp.stack([column_sums(item, row_part, col_weight, col_blocks) for item in tiles])
    checks = (local_sums * factor).reshape(3, 1, 1, col_blocks)
    return (tiles[0], tiles[1], tiles[2], checks)


def solution(mesh):
    finer = Mesh(
        mesh.devices.reshape(4, 2, 2, mesh.shape["pipe"], mesh.shape["tensor"]),
        ("dp_0", "dp_1", "dp_2", "pipe", "tensor"),
    )
    in_specs = (P(DP_PIPE_TENSOR, None), P(DP_PIPE_TENSOR, None), P(DP_PIPE_TENSOR, None), P(), P())
    out_specs = (
        P(("pipe", "tensor"), None),
        P(("pipe", "tensor"), None),
        P(("pipe", "tensor"), None),
        P(None, "pipe", "tensor", None),
    )
    return jax.shard_map(
        shards, mesh=finer, in_specs=in_specs, out_specs=out_specs, check_vma=False
    )
```

profile of v0, /device:TPU:1, one launch (start us, length us, event | category | flops | bytes accessed | tf_op | source)
XLA Modules:
  0.0 177.1 jit_solution(7908738768736243178)
XLA Ops:
  0.6 1.1 all_to_all.102
  1.7 0.7 copy.84
  2.4 10.1 %all-to-all-start = ((bf16[22,16,88]{2,0,1:T(8,128)(2,1)}), bf16[22,16,88]{2,0,1:T(8,128)(2,1)S(1)}, u32[]{:S(2)}, u32[]{:S(2)}) async-start(bf16[22,16,88]{2,0,1:T(8,128)(2,1)} %copy.84), calls=%async_computation | async-start | bytes 196608 | tf_op jit(solution)/shard_map/all_to_all | solution.py:56
  12.5 1.1 all_to_all.111
  13.6 0.7 copy.92
  14.3 4.2 %all-to-all-done = bf16[22,16,88]{2,0,1:T(8,128)(2,1)S(1)} async-done(((bf16[22,16,88]{2,0,1:T(8,128)(2,1)}), bf16[22,16,88]{2,0,1:T(8,128)(2,1)S(1)}, u32[]{:S(2)}, u32[]{:S(2)}) %all-to-all-start) | async-done | bytes 61984 | tf_op jit(solution)/shard_map/all_to_all | solution.py:56
  18.4 3.9 %all-to-all-start.3 = ((bf16[22,16,88]{2,0,1:T(8,128)(2,1)}), bf16[22,16,88]{2,0,1:T(8,128)(2,1)S(1)}, u32[]{:S(2)}, u32[]{:S(2)}) async-start(bf16[22,16,88]{2,0,1:T(8,128)(2,1)} %copy.92), calls=%async_computation.3 | async-start | bytes 196608 | tf_op jit(solution)/shard_map/all_to_all | solution.py:57
  22.3 0.2 all_to_all.120
  22.5 0.7 copy.100
  23.2 5.0 %all-to-all-done.3 = bf16[22,16,88]{2,0,1:T(8,128)(2,1)S(1)} async-done(((bf16[22,16,88]{2,0,1:T(8,128)(2,1)}), bf16[22,16,88]{2,0,1:T(8,128)(2,1)S(1)}, u32[]{:S(2)}, u32[]{:S(2)}) %all-to-all-start.3) | async-done | bytes 61984 | tf_op jit(solution)/shard_map/all_to_all | solution.py:57
  28.2 3.9 %all-to-all-start.6 = ((bf16[22,16,88]{2,0,1:T(8,128)(2,1)}), bf16[22,16,88]{2,0,1:T(8,128)(2,1)S(1)}, u32[]{:S(2)}, u32[]{:S(2)}) async-start(bf16[22,16,88]{2,0,1:T(8,128)(2,1)} %copy.100), calls=%async_computation.6 | async-start | bytes 196608 | tf_op jit(solution)/shard_map/all_to_all | solution.py:58
  32.1 0.7 copy.86
  32.8 5.2 %all-to-all-done.6 = bf16[22,16,88]{2,0,1:T(8,128)(2,1)S(1)} async-done(((bf16[22,16,88]{2,0,1:T(8,128)(2,1)}), bf16[22,16,88]{2,0,1:T(8,128)(2,1)S(1)}, u32[]{:S(2)}, u32[]{:S(2)}) %all-to-all-start.6) | async-done | bytes 61984 | tf_op jit(solution)/shard_map/all_to_all | solution.py:58
  38.0 6.6 %all-to-all-start.1 = ((bf16[8,2,22,88]{3,1,2,0:T(2,128)(2,1)}), bf16[8,2,22,88]{3,1,2,0:T(2,128)(2,1)S(1)}, u32[]{:S(2)}, u32[]{:S(2)}) async-start(bf16[8,2,22,88]{3,1,2,0:T(2,128)(2,1)} %copy.86), calls=%async_computation.1 | async-start | bytes 180224 | tf_op jit(solution)/shard_map/all_to_all | solution.py:65
  44.7 0.7 copy.94
  45.4 6.8 %all-to-all-done.1 = bf16[8,2,22,88]{3,1,2,0:T(2,128)(2,1)S(1)} async-done(((bf16[8,2,22,88]{3,1,2,0:T(2,128)(2,1)}), bf16[8,2,22,88]{3,1,2,0:T(2,128)(2,1)S(1)}, u32[]{:S(2)}, u32[]{:S(2)}) %all-to-all-start.1) | async-done | bytes 61984 | tf_op jit(solution)/shard_map/all_to_all | solution.py:65
  52.1 3.4 %all-to-all-start.4 = ((bf16[8,2,22,88]{3,1,2,0:T(2,128)(2,1)}), bf16[8,2,22,88]{3,1,2,0:T(2,128)(2,1)S(1)}, u32[]{:S(2)}, u32[]{:S(2)}) async-start(bf16[8,2,22,88]{3,1,2,0:T(2,128)(2,1)} %copy.94), calls=%async_computation.4 | async-start | bytes 180224 | tf_op jit(solution)/shard_map/all_to_all | solution.py:65
  55.5 0.7 copy.102
  56.2 6.8 %all-to-all-done.4 = bf16[8,2,22,88]{3,1,2,0:T(2,128)(2,1)S(1)} async-done(((bf16[8,2,22,88]{3,1,2,0:T(2,128)(2,1)}), bf16[8,2,22,88]{3,1,2,0:T(2,128)(2,1)S(1)}, u32[]{:S(2)}, u32[]{:S(2)}) %all-to-all-start.4) | async-done | bytes 61984 | tf_op jit(solution)/shard_map/all_to_all | solution.py:65
  63.0 3.4 %all-to-all-start.7 = ((bf16[8,2,22,88]{3,1,2,0:T(2,128)(2,1)}), bf16[8,2,22,88]{3,1,2,0:T(2,128)(2,1)S(1)}, u32[]{:S(2)}, u32[]{:S(2)}) async-start(bf16[8,2,22,88]{3,1,2,0:T(2,128)(2,1)} %copy.102), calls=%async_computation.7 | async-start | bytes 180224 | tf_op jit(solution)/shard_map/all_to_all | solution.py:65
  66.4 0.7 copy.88
  67.1 6.7 %all-to-all-done.7 = bf16[8,2,22,88]{3,1,2,0:T(2,128)(2,1)S(1)} async-done(((bf16[8,2,22,88]{3,1,2,0:T(2,128)(2,1)}), bf16[8,2,22,88]{3,1,2,0:T(2,128)(2,1)S(1)}, u32[]{:S(2)}, u32[]{:S(2)}) %all-to-all-start.7) | async-done | bytes 61984 | tf_op jit(solution)/shard_map/all_to_all | solution.py:65
  73.8 5.9 %all-to-all-start.2 = ((bf16[4,4,1,22,88]{4,1,3,2,0:T(4,128)(2,1)}), bf16[4,4,1,22,88]{4,1,3,2,0:T(4,128)(2,1)S(1)}, u32[]{:S(2)}, u32[]{:S(2)}) async-start(bf16[4,4,1,22,88]{4,1,3,2,0:T(4,128)(2,1)} %copy.88), calls=%async_computation.2 | async-start | bytes 180224 | tf_op jit(solution)/shard_map/all_to_all | solution.py:73
  79.7 0.7 copy.96
  80.4 6.3 %all-to-all-done.2 = bf16[4,4,1,22,88]{4,1,3,2,0:T(4,128)(2,1)S(1)} async-done(((bf16[4,4,1,22,88]{4,1,3,2,0:T(4,128)(2,1)}), bf16[4,4,1,22,88]{4,1,3,2,0:T(4,128)(2,1)S(1)}, u32[]{:S(2)}, u32[]{:S(2)}) %all-to-all-start.2) | async-done | bytes 61984 | tf_op jit(solution)/shard_map/all_to_all | solution.py:73
  86.7 3.3 %all-to-all-start.5 = ((bf16[4,4,1,22,88]{4,1,3,2,0:T(4,128)(2,1)}), bf16[4,4,1,22,88]{4,1,3,2,0:T(4,128)(2,1)S(1)}, u32[]{:S(2)}, u32[]{:S(2)}) async-start(bf16[4,4,1,22,88]{4,1,3,2,0:T(4,128)(2,1)} %copy.96), calls=%async_computation.5 | async-start | bytes 180224 | tf_op jit(solution)/shard_map/all_to_all | solution.py:73
  90.0 0.8 dynamic_slice.3
  90.8 0.7 copy.104
  91.7 3.8 %all_gather.27 = bf16[2,352,88]{1,2,0:T(8,128)(2,1)S(1)} all-gather(bf16[1,352,88]{1,2,0:T(8,128)(2,1)S(1)} %copy.90), channel_id=1, replica_groups=mesh['dp_0'=4,'dp_1'=2,'dp_2'=2,'pipe'=8,'tensor'=4] {'dp_1'}, dimensions={0}, use_global_device_ids=true | all-gather | bytes 185856 | tf_op jit(solution)/shard_map/all_gather | solution.py:25
  95.5 1.5 all-to-all-done.5
  97.0 5.1 %all-to-all-start.8 = ((bf16[4,4,1,22,88]{4,1,3,2,0:T(4,128)(2,1)}), bf16[4,4,1,22,88]{4,1,3,2,0:T(4,128)(2,1)S(1)}, u32[]{:S(2)}, u32[]{:S(2)}) async-start(bf16[4,4,1,22,88]{4,1,3,2,0:T(4,128)(2,1)} %copy.104), calls=%async_computation.8 | async-start | bytes 180224 | tf_op jit(solution)/shard_map/all_to_all | solution.py:73
  102.1 0.1 copy.98
  102.3 4.3 %all_gather.30 = bf16[2,352,88]{1,2,0:T(8,128)(2,1)S(1)} all-gather(bf16[1,352,88]{1,2,0:T(8,128)(2,1)S(1)} %copy.98), channel_id=1, replica_groups=mesh['dp_0'=4,'dp_1'=2,'dp_2'=2,'pipe'=8,'tensor'=4] {'dp_1'}, dimensions={0}, use_global_device_ids=true | all-gather | bytes 185856 | tf_op jit(solution)/shard_map/all_gather | solution.py:25
  106.5 10.5 %all_gather.31 = bf16[8,352,88]{1,2,0:T(8,128)(2,1)S(1)} all-gather(bf16[2,352,88]{1,2,0:T(8,128)(2,1)S(1)} %all_gather.30), channel_id=1, replica_groups=mesh['dp_0'=4,'dp_1'=2,'dp_2'=2,'pipe'=8,'tensor'=4] {'dp_0'}, dimensions={0}, use_global_device_ids=true | all-gather | bytes 619520 | tf_op jit(solution)/shard_map/all_gather | solution.py:25
  117.1 11.4 %all_gather.28 = bf16[8,352,88]{1,2,0:T(8,128)(2,1)S(1)} all-gather(bf16[2,352,88]{1,2,0:T(8,128)(2,1)S(1)} %all_gather.27), channel_id=1, replica_groups=mesh['dp_0'=4,'dp_1'=2,'dp_2'=2,'pipe'=8,'tensor'=4] {'dp_0'}, dimensions={0}, use_global_device_ids=true | all-gather | bytes 619520 | tf_op jit(solution)/shard_map/all_gather | solution.py:25
  128.4 15.4 %all_gather.29 = bf16[16,352,88]{1,2,0:T(8,128)(2,1)S(1)} all-gather(bf16[8,352,88]{1,2,0:T(8,128)(2,1)S(1)} %all_gather.28), channel_id=1, replica_groups=mesh['dp_0'=4,'dp_1'=2,'dp_2'=2,'pipe'=8,'tensor'=4] {'dp_2'}, dimensions={0}, use_global_device_ids=true | all-gather | bytes 1486848 | tf_op jit(solution)/shard_map/all_gather | solution.py:25
  143.9 1.9 %copy.108 = bf16[352,1408]{1,0:T(8,128)(2,1)} copy(bf16[352,1408]{0,1:T(8,128)(2,1)S(1)} %bitcast.77) | data formatting | bytes 1982464
  145.8 1.0 convolution_reduce_fusion.2
  146.8 2.6 %all_gather.32 = bf16[16,352,88]{1,2,0:T(8,128)(2,1)S(1)} all-gather(bf16[8,352,88]{1,2,0:T(8,128)(2,1)S(1)} %all_gather.31), channel_id=1, replica_groups=mesh['dp_0'=4,'dp_1'=2,'dp_2'=2,'pipe'=8,'tensor'=4] {'dp_2'}, dimensions={0}, use_global_device_ids=true | all-gather | bytes 1486848 | tf_op jit(solution)/shard_map/all_gather | solution.py:25
  149.5 1.9 %copy.109 = bf16[352,1408]{1,0:T(8,128)(2,1)} copy(bf16[352,1408]{0,1:T(8,128)(2,1)S(1)} %bitcast.79) | data formatting | bytes 1982464
  151.4 1.0 convolution_reduce_fusion.1
  152.6 3.8 %all_gather.33 = bf16[2,352,88]{1,2,0:T(8,128)(2,1)S(1)} all-gather(bf16[1,352,88]{1,2,0:T(8,128)(2,1)S(1)} %copy.106), channel_id=1, replica_groups=mesh['dp_0'=4,'dp_1'=2,'dp_2'=2,'pipe'=8,'tensor'=4] {'dp_1'}, dimensions={0}, use_global_device_ids=true | all-gather | bytes 185856 | tf_op jit(solution)/shard_map/all_gather | solution.py:25
  156.4 10.2 %all_gather.34 = bf16[8,352,88]{1,2,0:T(8,128)(2,1)S(1)} all-gather(bf16[2,352,88]{1,2,0:T(8,128)(2,1)S(1)} %all_gather.33), channel_id=1, replica_groups=mesh['dp_0'=4,'dp_1'=2,'dp_2'=2,'pipe'=8,'tensor'=4] {'dp_0'}, dimensions={0}, use_global_device_ids=true | all-gather | bytes 619520 | tf_op jit(solution)/shard_map/all_gather | solution.py:25
  166.6 6.7 %all_gather.35 = bf16[16,352,88]{1,2,0:T(8,128)(2,1)S(1)} all-gather(bf16[8,352,88]{1,2,0:T(8,128)(2,1)S(1)} %all_gather.34), channel_id=1, replica_groups=mesh['dp_0'=4,'dp_1'=2,'dp_2'=2,'pipe'=8,'tensor'=4] {'dp_2'}, dimensions={0}, use_global_device_ids=true | all-gather | bytes 1486848 | tf_op jit(solution)/shard_map/all_gather | solution.py:25
  173.4 1.0 convolution_reduce_fusion
  174.4 1.9 %copy.110 = bf16[352,1408]{1,0:T(8,128)(2,1)} copy(bf16[352,1408]{0,1:T(8,128)(2,1)S(1)} %bitcast.76) | data formatting | bytes 1982464
  176.3 0.1 bitcast_reduce_fusion.2
  176.5 0.6 maximum_multiply_fusion
  (23 shorter events, 0.8 us)
Async XLA Ops:
  0.6 21.7 %copy-start = (bf16[22,1408]{1,0:T(8,128)(2,1)S(1)}, bf16[22,1408]{1,0:T(8,128)(2,1)}, u32[]{:S(2)}) copy-start(bf16[22,1408]{1,0:T(8,128)(2,1)} %param.7) | copy-start | bytes 185860
  2.4 16.0 %all-to-all-start = ((bf16[22,16,88]{2,0,1:T(8,128)(2,1)}), bf16[22,16,88]{2,0,1:T(8,128)(2,1)S(1)}, u32[]{:S(2)}, u32[]{:S(2)}) async-start(bf16[22,16,88]{2,0,1:T(8,128)(2,1)} %copy.84), calls=%async_computation | async-start | bytes 196608 | tf_op jit(solution)/shard_map/all_to_all | solution.py:56
  18.4 9.8 %all-to-all-start.3 = ((bf16[22,16,88]{2,0,1:T(8,128)(2,1)}), bf16[22,16,88]{2,0,1:T(8,128)(2,1)S(1)}, u32[]{:S(2)}, u32[]{:S(2)}) async-start(bf16[22,16,88]{2,0,1:T(8,128)(2,1)} %copy.92), calls=%async_computation.3 | async-start | bytes 196608 | tf_op jit(solution)/shard_map/all_to_all | solution.py:57
  28.2 9.8 %all-to-all-start.6 = ((bf16[22,16,88]{2,0,1:T(8,128)(2,1)}), bf16[22,16,88]{2,0,1:T(8,128)(2,1)S(1)}, u32[]{:S(2)}, u32[]{:S(2)}) async-start(bf16[22,16,88]{2,0,1:T(8,128)(2,1)} %copy.100), calls=%async_computation.6 | async-start | bytes 196608 | tf_op jit(solution)/shard_map/all_to_all | solution.py:58
  38.0 14.1 %all-to-all-start.1 = ((bf16[8,2,22,88]{3,1,2,0:T(2,128)(2,1)}), bf16[8,2,22,88]{3,1,2,0:T(2,128)(2,1)S(1)}, u32[]{:S(2)}, u32[]{:S(2)}) async-start(bf16[8,2,22,88]{3,1,2,0:T(2,128)(2,1)} %copy.86), calls=%async_computation.1 | async-start | bytes 180224 | tf_op jit(solution)/shard_map/all_to_all | solution.py:65
  52.1 10.9 %all-to-all-start.4 = ((bf16[8,2,22,88]{3,1,2,0:T(2,128)(2,1)}), bf16[8,2,22,88]{3,1,2,0:T(2,128)(2,1)S(1)}, u32[]{:S(2)}, u32[]{:S(2)}) async-start(bf16[8,2,22,88]{3,1,2,0:T(2,128)(2,1)} %copy.94), calls=%async_computation.4 | async-start | bytes 180224 | tf_op jit(solution)/shard_map/all_to_all | solution.py:65
  63.0 10.8 %all-to-all-start.7 = ((bf16[8,2,22,88]{3,1,2,0:T(2,128)(2,1)}), bf16[8,2,22,88]{3,1,2,0:T(2,128)(2,1)S(1)}, u32[]{:S(2)}, u32[]{:S(2)}) async-start(bf16[8,2,22,88]{3,1,2,0:T(2,128)(2,1)} %copy.102), calls=%async_computation.7 | async-start | bytes 180224 | tf_op jit(solution)/shard_map/all_to_all | solution.py:65
  73.8 12.9 %all-to-all-start.2 = ((bf16[4,4,1,22,88]{4,1,3,2,0:T(4,128)(2,1)}), bf16[4,4,1,22,88]{4,1,3,2,0:T(4,128)(2,1)S(1)}, u32[]{:S(2)}, u32[]{:S(2)}) async-start(bf16[4,4,1,22,88]{4,1,3,2,0:T(4,128)(2,1)} %copy.88), calls=%async_computation.2 | async-start | bytes 180224 | tf_op jit(solution)/shard_map/all_to_all | solution.py:73
  86.7 10.3 %all-to-all-start.5 = ((bf16[4,4,1,22,88]{4,1,3,2,0:T(4,128)(2,1)}), bf16[4,4,1,22,88]{4,1,3,2,0:T(4,128)(2,1)S(1)}, u32[]{:S(2)}, u32[]{:S(2)}) async-start(bf16[4,4,1,22,88]{4,1,3,2,0:T(4,128)(2,1)} %copy.96), calls=%async_computation.5 | async-start | bytes 180224 | tf_op jit(solution)/shard_map/all_to_all | solution.py:73
  97.0 55.4 %all-to-all-start.8 = ((bf16[4,4,1,22,88]{4,1,3,2,0:T(4,128)(2,1)}), bf16[4,4,1,22,88]{4,1,3,2,0:T(4,128)(2,1)S(1)}, u32[]{:S(2)}, u32[]{:S(2)}) async-start(bf16[4,4,1,22,88]{4,1,3,2,0:T(4,128)(2,1)} %copy.104), calls=%async_computation.8 | async-start | bytes 180224 | tf_op jit(solution)/shard_map/all_to_all | solution.py:73
  174.4 1.9 %copy-start.1 = (f32[1408]{0:T(1024)S(1)}, f32[1408]{0:T(1024)}, u32[]{:S(2)}) copy-start(f32[1408]{0:T(1024)} %param.9) | copy-start | bytes 16900
where the time goes:
time: 178 us; the launch traced here: 177 us
  blocking collectives  68.7 us (39%)
  starting transfers between devices  45.5 us (26%)
  waiting for transfers between devices  42.5 us (24%)
  local copies, waits for them, and re-layouts  15.8 us (9%)
  matrix products  2.99 us (2%)
    all_gather x9, blocking collectives, gather_in_order(): blocks = lax.all_gather(blocks, axes[k], axis=0, tiled=True)  68.7 us
    all_to_all x3, waiting for transfers between devices, shards(): lax.all_to_all(for_sending(grouped), 'pipe', split_axis=0, concat_axis=2,...  20.2 us
    all_to_all x3, starting transfers between devices, shards(): lax.all_to_all(for_sending(routed), 'tensor', split_axis=0, concat_axis=2...  14.3 us
    all_to_all x3, starting transfers between devices, shards(): lax.all_to_all(for_sending(grouped), 'pipe', split_axis=0, concat_axis=2,...  13.4 us
    all_to_all x1, starting transfers between devices, shards(): lax.all_to_all(sources[0], DP, split_axis=1, concat_axis=0, tiled=True)  10.1 us
    all_to_all x3, waiting for transfers between devices, shards(): lax.all_to_all(for_sending(routed), 'tensor', split_axis=0, concat_axis=2...  7.87 us
    unnamed x7, local copies, waits for them, and re-layouts  5.68 us
    all_to_all x1, waiting for transfers between devices, shards(): lax.all_to_all(sources[2], DP, split_axis=1, concat_axis=0, tiled=True)  5.18 us
  transfers between devices with their start and end apart: 9, of which 8 were waited for; matrix products, arithmetic and copies ran while one was open for 7% of the time, Pallas kernels for 0%

commit v1 on v0

v1 whole, which is shorter than its diff:
```python
import jax
import jax.numpy as jnp
from jax import lax
from jax.experimental import pallas as pl
from jax.experimental.pallas import tpu as pltpu
from jax.sharding import PartitionSpec as P

MESH = pl.DeviceIdType.MESH
CHECK_COLS = 128
X_SLOT, Z_SLOT, OWN_SLOT, SLOTS = 16, 17, 19, 20


def kernel(
    w_ref, m_ref, v_ref, row_ref, col_ref, wo_ref, mo_ref, vo_ref, check_ref,
    held, row_part, in_sem, x_sem, z_sem, got_sem, send_sem,
):
    sources, tiles = (w_ref, m_ref, v_ref), (wo_ref, mo_ref, vo_ref)
    rows = w_ref.shape[0]
    width = w_ref.shape[1]
    tile_rows = wo_ref.shape[0]
    d, z, yh = lax.axis_index("dp"), lax.axis_index("pipe"), lax.axis_index("tensor")
    x, yl, c = d // 4, (d // 2) % 2, d % 2
    sign = 1 - 2 * c

    def at(x_, yl_, c_, z_=None, yh_=None):
        return {
            "dp": x_ * 4 + yl_ * 2 + c_,
            "pipe": z if z_ is None else z_,
            "tensor": yh if yh_ is None else yh_,
        }

    sends = []

    def send(src, dst, sem, to, condition=None):
        copy = pltpu.make_async_remote_copy(
            src_ref=src,
            dst_ref=dst,
            send_sem=send_sem.at[len(sends)],
            recv_sem=sem,
            device_id=to,
            device_id_type=MESH,
        )
        sends.append((condition, copy))
        if condition is None:
            copy.start()
        else:
            pl.when(condition)(copy.start)

    core_mate = at(x, yl, 1 - c)

    def arrive(ref, sem):
        pltpu.make_async_remote_copy(
            src_ref=ref, dst_ref=ref, send_sem=send_sem.at[0], recv_sem=sem,
            device_id=core_mate, device_id_type=MESH,
        ).wait_recv()

    x_to = (z + 8 - x - yl) % 4
    x_moves = x_to != x
    x_mate = at(x_to, yl, c)
    z_to = 2 * x_to + yl
    z_moves = z_to != z
    z_dest = at(x, yl, c, z_=z_to)
    even = z % 2 == yl
    quarter = (z // 2 + z % 2 + x) % 4
    y_place = 4 * quarter + yh
    y_dests = [at(x, yh % 2, yh // 2, yh_=2 * c + h) for h in range(2)]
    own = 4 * quarter + yl + 2 * c
    y_source = at(x, z % 2, yh // 2, yh_=yl + 2 * c)
    stays = jnp.logical_and(even, jnp.logical_and(yh == yl + 2 * c, c == yh // 2))

    barrier = pltpu.get_barrier_semaphore()
    y_mate = at(x, 1 - yl, c)
    x_next = {s: at((x + 4 + s * sign) % 4, yl, c) for s in (1, -1)}

    def greet(to):
        pl.semaphore_signal(barrier, inc=1, device_id=to, device_id_type=MESH)

    for to in (x_mate, y_source, y_mate, x_next[1], x_next[-1], core_mate):
        greet(to)

    @pl.when(even)
    def _():
        greet(at(x, yl, c, z_=quarter))
        greet(at(x, yl, c, z_=quarter + 4))

    loads = []
    for a in range(3):
        load = pltpu.make_async_copy(sources[a], held.at[a, OWN_SLOT], in_sem.at[a])
        load.start()
        loads.append(load)

    for j in range(tile_rows // rows // 4):

        @pl.when(yh == j)
        def _():
            row_part[...] = row_ref[:, j * tile_rows : (j + 1) * tile_rows]

    pl.semaphore_wait(barrier, 6 + 2 * even.astype(jnp.int32))

    for a in range(3):
        loads[a].wait()
        send(held.at[a, OWN_SLOT], held.at[a, X_SLOT], x_sem.at[a], x_mate, x_moves)
    x_slot = jnp.where(x_moves, X_SLOT, OWN_SLOT)
    half = z // 4
    for a in range(3):

        @pl.when(x_moves)
        def _():
            arrive(held.at[a, X_SLOT], x_sem.at[a])

        send(held.at[a, x_slot], held.at[a, Z_SLOT + half], z_sem.at[half, a], z_dest, z_moves)
    here = [jnp.logical_and(even, quarter + 4 * h == z) for h in range(2)]
    away = [jnp.logical_and(even, quarter + 4 * h != z) for h in range(2)]
    z_slot = [jnp.where(here[h], x_slot, Z_SLOT + h) for h in range(2)]
    for a in range(3):
        for h in range(2):

            @pl.when(away[h])
            def _():
                arrive(held.at[a, Z_SLOT + h], z_sem.at[h, a])

            mine = jnp.logical_and(stays, yh % 2 == h)
            send(
                held.at[a, z_slot[h]], held.at[a, y_place], got_sem.at[a, y_place], y_dests[h],
                jnp.logical_and(even, jnp.logical_not(mine)),
            )
    own_slot = jnp.where(stays, jnp.where(yh % 2 == 0, z_slot[0], z_slot[1]), own)

    def slot(dx, other):
        row = 1 - yl if other else yl
        return 4 * ((z // 2 + z % 2 + x + 4 + dx * sign) % 4) + row + 2 * c

    def pass_on(a, dx, other, to, wait=True):
        k = slot(dx, other)
        src = k
        if dx == 0 and not other:
            src = own_slot

            @pl.when(jnp.logical_not(stays))
            def _():
                arrive(held.at[a, k], got_sem.at[a, k])

        else:
            arrive(held.at[a, k], got_sem.at[a, k])
        for dest in to:
            send(held.at[a, src], held.at[a, k], got_sem.at[a, k], dest)

    xs = (x_next[1], x_next[-1])
    pass_on(0, 0, 0, (*xs, y_mate, core_mate))
    pass_on(1, 0, 0, (y_mate, *xs, core_mate))
    pass_on(2, 0, 0, (y_mate, *xs, core_mate))
    pass_on(0, -1, 0, (x_next[1], y_mate, core_mate))
    pass_on(1, 0, 1, (*xs, core_mate))
    pass_on(2, 0, 1, (*xs, core_mate))
    pass_on(0, 1, 0, (y_mate, core_mate))
    for a in (1, 2):
        pass_on(a, -1, 0, (x_next[1], core_mate))
    for a in (1, 2):
        pass_on(a, -1, 1, (x_next[1], core_mate))
    pass_on(0, 2, 0, (y_mate, core_mate))
    for dx in (0, -1, 1):
        pass_on(0, dx, 1, (core_mate,))
    for other in (0, 1):
        for a in (1, 2):
            pass_on(a, 1, other, (core_mate,))
    for other in (0, 1):
        for a in (1, 2):
            pass_on(a, 2, other, (core_mate,))
    pass_on(0, 2, 1, (core_mate,))

    for a in range(3):

        @pl.when(stays)
        def _():
            held[a, own] = held[a, own_slot]

    part = row_part[...]
    high = part.astype(jnp.bfloat16).astype(jnp.float32)
    middle = (part - high).astype(jnp.bfloat16).astype(jnp.float32)
    low = part - high - middle
    line = lax.broadcasted_iota(jnp.int32, (8, tile_rows), 0)
    left = jnp.where(line == 0, high, jnp.where(line == 1, middle, jnp.where(line == 2, low, 0.0)))
    left = left.astype(jnp.bfloat16)
    factor = float(tile_rows * CHECK_COLS) ** (-0.5)
    weight = col_ref[...] * factor
    lane = lax.broadcasted_iota(jnp.int32, (1, CHECK_COLS), 1)
    for a in range(3):
        for k in range(16):

            @pl.when(c != (k % 4) // 2)
            def _():
                arrive(held.at[a, k], got_sem.at[a, k])

            tiles[a][k * rows : (k + 1) * rows, :] = held[a, k]
        mixed = jnp.dot(left, tiles[a][...], preferred_element_type=jnp.float32)
        mixed = jnp.sum(mixed, axis=0, keepdims=True) * weight
        sums = jnp.zeros((1, CHECK_COLS), jnp.float32)
        for e in range(width // CHECK_COLS):
            piece = mixed[:, e * CHECK_COLS : (e + 1) * CHECK_COLS]
            sums = jnp.where(lane == e, jnp.sum(piece, axis=1, keepdims=True), sums)
        check_ref[a, 0] = sums[:, : width // CHECK_COLS]

    for condition, copy in sends:
        if condition is None:
            copy.wait_send()
        else:
            pl.when(condition)(copy.wait_send)


def shards(weights, first_moment, second_moment, row_weight, col_weight):
    rows, width = weights.shape
    tile_rows = rows * 16
    whole = pl.BlockSpec(memory_space=pltpu.VMEM)
    tile = jax.ShapeDtypeStruct((tile_rows, width), jnp.bfloat16)
    return pl.pallas_call(
        kernel,
        out_shape=(
            tile, tile, tile,
            jax.ShapeDtypeStruct((3, 1, 1, width // CHECK_COLS), jnp.float32),
        ),
        in_specs=[pl.BlockSpec(memory_space=pl.ANY)] * 3 + [whole] * 2,
        out_specs=(whole,) * 4,
        scratch_shapes=[
            pltpu.VMEM((3, SLOTS, rows, width), jnp.bfloat16),
            pltpu.VMEM((1, tile_rows), jnp.float32),
            pltpu.SemaphoreType.DMA((3,)),
            pltpu.SemaphoreType.DMA((3,)),
            pltpu.SemaphoreType.DMA((2, 3)),
            pltpu.SemaphoreType.DMA((3, 16)),
            pltpu.SemaphoreType.DMA((64,)),
        ],
        compiler_params=pltpu.CompilerParams(collective_id=0, has_side_effects=True),
    )(
        weights, first_moment, second_moment,
        row_weight.reshape(1, width), col_weight.reshape(1, width),
    )


def solution(mesh):
    flat = P(("dp", "pipe", "tensor"), None)
    tile = P(("pipe", "tensor"), None)
    return jax.shard_map(
        shards,
        mesh=mesh,
        in_specs=(flat, flat, flat, P(), P()),
        out_specs=(tile, tile, tile, P(None, "pipe", "tensor", None)),
        check_vma=False,
    )
```

time: 178 us -> 58.9 us (0.33)
  blocking collectives: 68.7 us -> 0 us
  Pallas kernels: 0 us -> 50.6 us
  starting transfers between devices: 45.5 us -> 0 us
  waiting for transfers between devices: 42.5 us -> 0 us
  local copies, waits for them, and re-layouts: 15.8 us -> 7.29 us
  matrix products: 2.99 us -> 0 us
    all_gather x9 -> x0, blocking collectives: 68.7 us -> none  [gather_in_order(): blocks = lax.all_gather(blocks, axes[k], axis=0, tiled=True)]
    pallas_call x0 -> x1, Pallas kernels: none -> 50.6 us  [shards(): pl.pallas_call(kernel, out_shape=(tile, tile, tile, jax.ShapeDtypeStruct(...]
    all_to_all x9 -> x0, starting transfers between devices: 45.5 us -> none  [the longest x3 14.3 us: shards(): lax.all_to_all(for_sending(routed), 'tensor', split_axis=0, concat_axis=2...]
    all_to_all x9 -> x0, waiting for transfers between devices: 42.5 us -> none  [the longest x3 20.2 us: shards(): lax.all_to_all(for_sending(grouped), 'pipe', split_axis=0, concat_axis=2,...]
    all_to_all x15 -> x0, local copies, waits for them, and re-layouts: 4.5 us -> none  [the longest x3 1.77 us: shards(): lax.all_to_all(sources[0], DP, split_axis=1, concat_axis=0, tiled=True)]
    dot_general x3 -> x0, matrix products: 2.99 us -> none  [column_sums(): jnp.dot(row_part[None, :], data.astype(jnp.float32), precision=lax.Precis...]
    reshape x6 -> x2, local copies, waits for them, and re-layouts: 4.12 us -> 1.9 us  [the longest x1 1.3 us: shards(): row_weight.reshape(1, width)]
    unnamed x7 -> x12, local copies, waits for them, and re-layouts: 5.68 us -> 5.39 us
  transfers between devices with their start and end apart: 9 -> 0, of which waited for: 8 -> 0; matrix products, arithmetic and copies ran while one was open for 7% -> 0% of each run, Pallas kernels for 0% -> 0%
where the time goes in v1:
time: 58.9 us; the launch traced here: 58.6 us
  Pallas kernels  50.6 us (86%)
  local copies, waits for them, and re-layouts  7.29 us (12%)
  between operations  0.66 us (1%)
    pallas_call x1, Pallas kernels, shards(): pl.pallas_call(kernel, out_shape=(tile, tile, tile, jax.ShapeDtypeStruct(...  50.6 us
    unnamed x12, local copies, waits for them, and re-layouts  5.39 us
    reshape x1, local copies, waits for them, and re-layouts, shards(): row_weight.reshape(1, width)  1.3 us

profile of v1, /device:TPU:1, one launch (start us, length us, event | category | flops | bytes accessed | tf_op | source)
XLA Modules:
  0.0 58.6 jit_solution(3773303901159919079)
XLA Ops:
  0.6 0.0 copy-start.2
  0.6 1.3 %reshape.14.row_ref = f32[1,1408]{1,0:T(1,128)} reshape(f32[1408]{0:T(1024)} %param.8) | data formatting | bytes 11264 | tf_op jit(solution)/shard_map/reshape | solution.py:235
  1.9 0.0 copy-done.2
  1.9 0.6 %reshape.15.col_ref = f32[1,1408]{1,0:T(1,128)} reshape(f32[1408]{0:T(1024)S(1)} %copy-done.2) | data formatting | bytes 11264 | tf_op jit(solution)/shard_map/reshape | solution.py:235
  2.5 50.6 %shard_map.84 = (bf16[352,1408]{1,0:T(8,128)(2,1)}, bf16[352,1408]{1,0:T(8,128)(2,1)}, bf16[352,1408]{1,0:T(8,128)(2,1)}, f32[3,1,1,11]{3,2,1,0:T(1,128)}) custom-call(bf16[22,1408]{1,0:T(8,128)(2,1)} %w_ref.1, bf16[22,1408]{1,0:T(8,128)(2,1)} %m_ref.1, bf16[22,1408]{1,0:T(8,128)(2,1)} %v_ref.1, f32[1,1408]{1,0:T(1,128)} %reshape.14.row_ref, ...), custom_call_target="tpu_custom_call" | custom-call | tf_op jit(solution)/shard_map/pallas_call | solution.py:215
  53.2 0.0 copy-start.1
  53.2 2.3 %copy.13 = bf16[352,1408]{1,0:T(8,128)(2,1)} copy(bf16[352,1408]{1,0:T(8,128)(2,1)} %get-tuple-element.8) | data formatting | bytes 1982464
  55.5 0.0 copy-done.1
  55.5 0.0 copy-start
  55.5 0.9 %copy.14 = bf16[352,1408]{1,0:T(8,128)(2,1)} copy(bf16[352,1408]{1,0:T(8,128)(2,1)S(1)} %copy-done.1) | data formatting | bytes 1982464
  56.4 0.6 %copy-done = bf16[352,1408]{1,0:T(8,128)(2,1)S(1)} copy-done((bf16[352,1408]{1,0:T(8,128)(2,1)S(1)}, bf16[352,1408]{1,0:T(8,128)(2,1)}, u32[]{:S(2)}) %copy-start) | copy-done | bytes 991256
  57.1 0.0 copy-start.3
  57.1 0.9 %copy.15 = bf16[352,1408]{1,0:T(8,128)(2,1)} copy(bf16[352,1408]{1,0:T(8,128)(2,1)S(1)} %copy-done) | data formatting | bytes 1982464
  58.0 0.0 copy-done.3
  58.0 0.6 copy.16
Async XLA Ops:
  0.6 1.3 %copy-start.2 = (f32[1408]{0:T(1024)S(1)}, f32[1408]{0:T(1024)}, u32[]{:S(2)}) copy-start(f32[1408]{0:T(1024)} %param.9) | copy-start | bytes 16900
  53.2 2.3 %copy-start.1 = (bf16[352,1408]{1,0:T(8,128)(2,1)S(1)}, bf16[352,1408]{1,0:T(8,128)(2,1)}, u32[]{:S(2)}) copy-start(bf16[352,1408]{1,0:T(8,128)(2,1)} %get-tuple-element.9) | copy-start | bytes 2973700
  55.5 1.6 %copy-start = (bf16[352,1408]{1,0:T(8,128)(2,1)S(1)}, bf16[352,1408]{1,0:T(8,128)(2,1)}, u32[]{:S(2)}) copy-start(bf16[352,1408]{1,0:T(8,128)(2,1)} %get-tuple-element.10) | copy-start | bytes 2973700
  57.1 1.0 %copy-start.3 = (f32[3,1,1,11]{3,2,1,0:T(1,128)S(1)}, f32[3,1,1,11]{3,2,1,0:T(1,128)}, u32[]{:S(2)}) copy-start(f32[3,1,1,11]{3,2,1,0:T(1,128)} %get-tuple-element.11) | copy-start | bytes 400

commit v2 on v1

v2 whole, which is shorter than its diff:
```python
import jax
import jax.numpy as jnp
from jax import lax
from jax.experimental import pallas as pl
from jax.experimental.pallas import tpu as pltpu
from jax.sharding import PartitionSpec as P

MESH = pl.DeviceIdType.MESH
CHECK_COLS = 128
X_SLOT, Z_SLOT, OWN_SLOT, SLOTS = 16, 17, 19, 20


def chunks_of(width):
    return [(a, slice(0, width)) for a in range(3)]


def kernel(
    w_ref, m_ref, v_ref, row_ref, col_ref, wo_ref, mo_ref, vo_ref, check_ref,
    held, row_all, col_all, row_part, in_sem, x_sem, z_sem, got_sem, send_sem,
):
    sources, tiles = (w_ref, m_ref, v_ref), (wo_ref, mo_ref, vo_ref)
    rows, width = w_ref.shape
    tile_rows = wo_ref.shape[0]
    chunks = chunks_of(width)
    d, z, yh = lax.axis_index("dp"), lax.axis_index("pipe"), lax.axis_index("tensor")
    x, yl, c = d // 4, (d // 2) % 2, d % 2
    sign = 1 - 2 * c

    def at(x_, yl_, c_, z_=None, yh_=None):
        return {
            "dp": x_ * 4 + yl_ * 2 + c_,
            "pipe": z if z_ is None else z_,
            "tensor": yh if yh_ is None else yh_,
        }

    core_mate, y_mate = at(x, yl, 1 - c), at(x, 1 - yl, c)
    x_next = {s: at((x + 4 + s * sign) % 4, yl, c) for s in (1, -1)}
    sends = []

    def piece(i, slot):
        a, columns = chunks[i]
        return held.at[a, slot, :, columns]

    def send(i, src, dst, sem, to, condition=None):
        copy = pltpu.make_async_remote_copy(
            src_ref=piece(i, src),
            dst_ref=piece(i, dst),
            send_sem=send_sem.at[len(sends)],
            recv_sem=sem,
            device_id=to,
            device_id_type=MESH,
        )
        sends.append((condition, copy))
        if condition is None:
            copy.start()
        else:
            pl.when(condition)(copy.start)

    def arrive(i, slot, sem, condition=None):
        copy = pltpu.make_async_remote_copy(
            src_ref=piece(i, slot), dst_ref=piece(i, slot), send_sem=send_sem.at[0],
            recv_sem=sem, device_id=core_mate, device_id_type=MESH,
        )
        if condition is None:
            copy.wait_recv()
        else:
            pl.when(condition)(copy.wait_recv)

    x_to = (z + 8 - x - yl) % 4
    x_moves = x_to != x
    x_mate = at(x_to, yl, c)
    z_to = 2 * x_to + yl
    z_moves = z_to != z
    z_dest = at(x, yl, c, z_=z_to)
    half = z // 4
    even = z % 2 == yl
    quarter = (z // 2 + z % 2 + x) % 4
    y_place = 4 * quarter + yh
    special = yh % 2
    own_half = c == yh // 2

    def y_dest(h, row):
        return at(x, row, yh // 2, yh_=2 * c + h)

    own = [4 * quarter + 2 * c + u for u in range(2)]
    y_source = [at(x, z % 2, yh // 2, yh_=2 * c + u) for u in range(2)]
    stays = [jnp.logical_and(even, jnp.logical_and(special == u, own_half)) for u in range(2)]
    handed = [
        jnp.logical_and(even, jnp.logical_and(special == u, jnp.logical_not(own_half))) for u in range(2)
    ]
    hands_on = [
        jnp.logical_and(
            jnp.logical_not(even), jnp.logical_and(special == u, jnp.logical_not(own_half))
        )
        for u in range(2)
    ]

    barrier = pltpu.get_barrier_semaphore()

    def greet(to):
        pl.semaphore_signal(barrier, inc=1, device_id=to, device_id_type=MESH)

    @pl.when(even)
    def _():
        greet(at(x, yl, c, z_=quarter))
        greet(at(x, yl, c, z_=quarter + 4))

    for to in (x_mate, x_next[1], x_next[-1], core_mate):
        greet(to)
    for u in range(2):
        direct = jnp.logical_not(jnp.logical_and(even, special == u))
        pl.when(direct)(lambda u=u: greet(y_source[u]))
        pl.when(handed[u])(lambda: greet(y_mate))

    loads = []
    for i in range(len(chunks)):
        a, columns = chunks[i]
        load = pltpu.make_async_copy(sources[a].at[:, columns], piece(i, OWN_SLOT), in_sem.at[i])
        load.start()
        loads.append(load)

    weight_loads = [
        pltpu.make_async_copy(row_ref, row_all, in_sem.at[len(chunks)]),
        pltpu.make_async_copy(col_ref, col_all, in_sem.at[len(chunks) + 1]),
    ]
    for load in weight_loads:
        load.start()

    count = 5 + 3 * even.astype(jnp.int32) + jnp.logical_or(hands_on[0], hands_on[1]).astype(jnp.int32)
    pl.semaphore_wait(barrier, count)

    each = range(len(chunks))
    for i in each:
        loads[i].wait()
        send(i, OWN_SLOT, X_SLOT, x_sem.at[i], x_mate, x_moves)
    x_slot = jnp.where(x_moves, X_SLOT, OWN_SLOT)
    for i in each:
        arrive(i, X_SLOT, x_sem.at[i], x_moves)
        send(i, x_slot, Z_SLOT + half, z_sem.at[half, i], z_dest, z_moves)
    away = [jnp.logical_and(even, quarter + 4 * h != z) for h in range(2)]
    z_slot = [jnp.where(quarter + 4 * h == z, x_slot, Z_SLOT + h) for h in range(2)]
    for i in each:
        for h in range(2):
            arrive(i, Z_SLOT + h, z_sem.at[h, i], away[h])
            got = got_sem.at[i, y_place]
            send(i, z_slot[h], y_place, got, y_dest(h, 1 - yl), even)
            normal = jnp.logical_and(even, special != h)
            send(i, z_slot[h], y_place, got, y_dest(h, yl), normal)
    own_slot = [jnp.where(stays[u], z_slot[u], own[u]) for u in range(2)]

    def mine(i):
        for u in range(2):
            got = got_sem.at[i, own[u]]
            arrive(i, own[u], got, jnp.logical_not(stays[u]))
            for to in (x_next[1], x_next[-1]):
                send(i, own_slot[u], own[u], got, to)
            send(i, own[u], own[u], got, y_mate, hands_on[u])
            send(i, own_slot[u], own[u], got, core_mate)

    def theirs(i, dx):
        for u in range(2):
            k = 4 * ((quarter + 4 + dx * sign) % 4) + 2 * c + u
            got = got_sem.at[i, k]
            arrive(i, k, got)
            if dx == -1:
                send(i, k, k, got, x_next[1])
            send(i, k, k, got, core_mate)

    for i in range(len(chunks) + 2):
        if i < len(chunks):
            mine(i)
        if 0 <= i - 1 < len(chunks):
            theirs(i - 1, -1)
            theirs(i - 1, 1)
        if 0 <= i - 2 < len(chunks):
            theirs(i - 2, 2)

    for u in range(2):

        @pl.when(stays[u])
        def _():
            for a in range(3):
                held[a, own[u]] = held[a, own_slot[u]]

    for load in weight_loads:
        load.wait()
    for j in range(width // tile_rows):

        @pl.when(yh == j)
        def _():
            row_part[0] = row_all[pl.ds(j * tile_rows, tile_rows)]
    part = row_part[...]
    high = part.astype(jnp.bfloat16).astype(jnp.float32)
    middle = (part - high).astype(jnp.bfloat16).astype(jnp.float32)
    low = part - high - middle
    line = lax.broadcasted_iota(jnp.int32, (8, tile_rows), 0)
    left = jnp.where(line == 0, high, jnp.where(line == 1, middle, jnp.where(line == 2, low, 0.0)))
    left = left.astype(jnp.bfloat16)
    factor = float(tile_rows * CHECK_COLS) ** (-0.5)
    weight = col_all[...].reshape(1, width) * factor
    lane = lax.broadcasted_iota(jnp.int32, (1, CHECK_COLS), 1)
    for a in range(3):
        for k in range(16):
            for i in each:
                if chunks[i][0] == a:
                    arrive(i, k, got_sem.at[i, k], c != (k % 4) // 2)
            tiles[a][k * rows : (k + 1) * rows, :] = held[a, k]
        mixed = jnp.dot(left, tiles[a][...], preferred_element_type=jnp.float32)
        mixed = jnp.sum(mixed, axis=0, keepdims=True) * weight
        sums = jnp.zeros((1, CHECK_COLS), jnp.float32)
        for e in range(width // CHECK_COLS):
            part_sum = jnp.sum(mixed[:, e * CHECK_COLS : (e + 1) * CHECK_COLS], axis=1, keepdims=True)
            sums = jnp.where(lane == e, part_sum, sums)
        check_ref[a, 0] = sums[:, : width // CHECK_COLS]

    for condition, copy in sends:
        if condition is None:
            copy.wait_send()
        else:
            pl.when(condition)(copy.wait_send)


def store(*refs):
    n = len(refs) // 2
    ins, outs, sem = refs[:n], refs[n : 2 * n], refs[2 * n]
    copies = [pltpu.make_async_copy(ins[i], outs[i], sem.at[i]) for i in range(n)]
    for copy in copies:
        copy.start()
    for copy in copies:
        copy.wait()


def shards(weights, first_moment, second_moment, row_weight, col_weight):
    rows, width = weights.shape
    tile_rows = rows * 16
    n = len(chunks_of(width))
    whole = pl.BlockSpec(memory_space=pltpu.VMEM)
    tile = ((tile_rows, width), jnp.bfloat16)
    check = ((3, 1, 1, width // CHECK_COLS), jnp.float32)
    made = pl.pallas_call(
        kernel,
        out_shape=(pltpu.VMEM(*tile),) * 3 + (pltpu.VMEM(*check),),
        in_specs=[pl.BlockSpec(memory_space=pltpu.HBM)] * 5,
        out_specs=(whole,) * 4,
        scratch_shapes=[
            pltpu.VMEM((3, SLOTS, rows, width), jnp.bfloat16),
            pltpu.VMEM((width,), jnp.float32),
            pltpu.VMEM((width,), jnp.float32),
            pltpu.VMEM((1, tile_rows), jnp.float32),
            pltpu.SemaphoreType.DMA((n + 2,)),
            pltpu.SemaphoreType.DMA((n,)),
            pltpu.SemaphoreType.DMA((2, n)),
            pltpu.SemaphoreType.DMA((n, 16)),
            pltpu.SemaphoreType.DMA((n * 24,)),
        ],
        compiler_params=pltpu.CompilerParams(
            collective_id=0, has_side_effects=True, vmem_limit_bytes=60 * 2**20
        ),
    )(weights, first_moment, second_moment, row_weight, col_weight)
    return pl.pallas_call(
        store,
        out_shape=(jax.ShapeDtypeStruct(*tile),) * 3 + (jax.ShapeDtypeStruct(*check),),
        in_specs=[whole] * 4,
        out_specs=(pl.BlockSpec(memory_space=pltpu.HBM),) * 4,
        scratch_shapes=[pltpu.SemaphoreType.DMA((4,))],
        compiler_params=pltpu.CompilerParams(vmem_limit_bytes=2**20),
    )(*made)


def solution(mesh):
    flat = P(("dp", "pipe", "tensor"), None)
    tile = P(("pipe", "tensor"), None)
    return jax.shard_map(
        shards,
        mesh=mesh,
        in_specs=(flat, flat, flat, P(), P()),
        out_specs=(tile, tile, tile, P(None, "pipe", "tensor", None)),
        check_vma=False,
    )
```

time: 58.9 us -> 52.4 us (0.89)
  local copies, waits for them, and re-layouts: 7.29 us -> 0 us
  Pallas kernels: 50.6 us -> 51.6 us
    unnamed x12 -> x0, local copies, waits for them, and re-layouts: 5.39 us -> none
    reshape x2 -> x0, local copies, waits for them, and re-layouts: 1.9 us -> none  [the longest x1 1.3 us: shards(): row_weight.reshape(1, width)]
    pallas_call x1 -> x2, Pallas kernels: 50.6 us -> 51.6 us  [the longest x1 50 us: shards(): pl.pallas_call(kernel, out_shape=(pltpu.VMEM(*tile),) * 3 + (pltpu.VMEM(*...]
where the time goes in v2:
time: 52.4 us; the launch traced here: 52.3 us
  Pallas kernels  51.6 us (98%)
  between operations  0.64 us (1%)
    pallas_call x1, Pallas kernels, shards(): pl.pallas_call(kernel, out_shape=(pltpu.VMEM(*tile),) * 3 + (pltpu.VMEM(*...  50 us
    pallas_call x1, Pallas kernels, shards(): pl.pallas_call(store, out_shape=(jax.ShapeDtypeStruct(*tile),) * 3 + (jax...  1.64 us

profile of v2, /device:TPU:1, one launch (start us, length us, event | category | flops | bytes accessed | tf_op | source)
XLA Modules:
  0.0 52.3 jit_solution(12565118972136193141)
XLA Ops:
  0.6 50.0 %shard_map.84 = (bf16[352,1408]{1,0:T(8,128)(2,1)S(1)}, bf16[352,1408]{1,0:T(8,128)(2,1)S(1)}, bf16[352,1408]{1,0:T(8,128)(2,1)S(1)}, f32[3,1,1,11]{3,2,1,0:T(1,128)S(1)}) custom-call(bf16[22,1408]{1,0:T(8,128)(2,1)} %w_ref.1, bf16[22,1408]{1,0:T(8,128)(2,1)} %m_ref.1, bf16[22,1408]{1,0:T(8,128)(2,1)} %v_ref.1, f32[1408]{0:T(1024)} %row_ref.1, f32[1408]{0:T(1024)} %col_ref.1), custom_call_target="tpu_custom_call" | custom-call | tf_op jit(solution)/shard_map/pallas_call | solution.py:240
  50.6 1.6 %shard_map.85 = (bf16[352,1408]{1,0:T(8,128)(2,1)}, bf16[352,1408]{1,0:T(8,128)(2,1)}, bf16[352,1408]{1,0:T(8,128)(2,1)}, f32[3,1,1,11]{3,2,1,0:T(1,128)}) custom-call(bf16[352,1408]{1,0:T(8,128)(2,1)S(1)} %get-tuple-element.8.refs_0_, bf16[352,1408]{1,0:T(8,128)(2,1)S(1)} %get-tuple-element.9.refs_1_, bf16[352,1408]{1,0:T(8,128)(2,1)S(1)} %get-tuple-element.10.refs_2_, ...), custom_call_target="tpu_custom_call" | custom-call | tf_op jit(solution)/shard_map/pallas_call | solution.py:260

commit v3 on v2

--- a/solution.py
+++ b/solution.py
@@ -8,6 +8,7 @@
 MESH = pl.DeviceIdType.MESH
 CHECK_COLS = 128
 X_SLOT, Z_SLOT, OWN_SLOT, SLOTS = 16, 17, 19, 20
+ONE_ROW = (0,)
 
 
 def chunks_of(width):
@@ -16,7 +17,7 @@
 
 def kernel(
     w_ref, m_ref, v_ref, row_ref, col_ref, wo_ref, mo_ref, vo_ref, check_ref,
-    held, row_all, col_all, row_part, in_sem, x_sem, z_sem, got_sem, send_sem,
+    held, row_all, col_all, row_part, in_sem, x_sem, z_sem, got_sem, send_sem, z_ready,
 ):
     sources, tiles = (w_ref, m_ref, v_ref), (wo_ref, mo_ref, vo_ref)
     rows, width = w_ref.shape
@@ -66,51 +67,46 @@
         else:
             pl.when(condition)(copy.wait_recv)
 
-    x_to = (z + 8 - x - yl) % 4
+    x_to = (z + 8 - x - yl + 2 * c) % 4
     x_moves = x_to != x
     x_mate = at(x_to, yl, c)
     z_to = 2 * x_to + yl
-    z_moves = z_to != z
     z_dest = at(x, yl, c, z_=z_to)
     half = z // 4
     even = z % 2 == yl
-    quarter = (z // 2 + z % 2 + x) % 4
-    y_place = 4 * quarter + yh
+    came = (z // 2 + z % 2 + x + 2 * c) % 4
+    quarter = (z // 2 + z % 2 + x + 2 * (yh // 2)) % 4
+    y_place = 4 * came + yh
     special = yh % 2
     own_half = c == yh // 2
 
     def y_dest(h, row):
         return at(x, row, yh // 2, yh_=2 * c + h)
 
-    own = [4 * quarter + 2 * c + u for u in range(2)]
-    y_source = [at(x, z % 2, yh // 2, yh_=2 * c + u) for u in range(2)]
-    stays = [jnp.logical_and(even, jnp.logical_and(special == u, own_half)) for u in range(2)]
-    handed = [
-        jnp.logical_and(even, jnp.logical_and(special == u, jnp.logical_not(own_half))) for u in range(2)
-    ]
-    hands_on = [
-        jnp.logical_and(
-            jnp.logical_not(even), jnp.logical_and(special == u, jnp.logical_not(own_half))
-        )
-        for u in range(2)
-    ]
+    order = (1 - special, special)
+    own = [4 * quarter + 2 * c + u for u in order]
+    y_source = [at(x, z % 2, yh // 2, yh_=2 * c + u) for u in order]
+    stays = jnp.logical_and(even, own_half)
+    handed = jnp.logical_and(even, jnp.logical_not(own_half))
+    hands_on = jnp.logical_not(jnp.logical_or(even, own_half))
+    one_stays = jnp.logical_and(stays, special == yl)
+    one_far = jnp.logical_and(handed, special == yl)
 
     barrier = pltpu.get_barrier_semaphore()
 
     def greet(to):
         pl.semaphore_signal(barrier, inc=1, device_id=to, device_id_type=MESH)
 
-    @pl.when(even)
-    def _():
-        greet(at(x, yl, c, z_=quarter))
-        greet(at(x, yl, c, z_=quarter + 4))
-
+    for h in range(2):
+        z_from = came + 4 * h
+        pl.when(jnp.logical_and(even, z_from > z))(lambda z_from=z_from: greet(at(x, yl, c, z_=z_from)))
+    pl.when(z_to > z)(lambda: greet(z_dest))
     for to in (x_mate, x_next[1], x_next[-1], core_mate):
         greet(to)
-    for u in range(2):
-        direct = jnp.logical_not(jnp.logical_and(even, special == u))
-        pl.when(direct)(lambda u=u: greet(y_source[u]))
-        pl.when(handed[u])(lambda: greet(y_mate))
+    greet(y_source[0])
+    pl.when(jnp.logical_not(even))(lambda: greet(y_source[1]))
+    greet(y_mate)
+    pl.when(one_far)(lambda: greet(y_source[1]))
 
     loads = []
     for i in range(len(chunks)):
@@ -126,80 +122,115 @@
     for load in weight_loads:
         load.start()
 
-    count = 5 + 3 * even.astype(jnp.int32) + jnp.logical_or(hands_on[0], hands_on[1]).astype(jnp.int32)
+    count = 5 + 3 * even.astype(jnp.int32) + one_far.astype(jnp.int32)
+    count = count + (z_to < z).astype(jnp.int32)
+    for h in range(2):
+        count = count + jnp.logical_and(even, came + 4 * h < z).astype(jnp.int32)
     pl.semaphore_wait(barrier, count)
+    for h in range(2):
+        z_from = came + 4 * h
+
+        @pl.when(jnp.logical_and(even, z_from < z))
+        def _():
+            pl.semaphore_signal(
+                z_ready, inc=1, device_id=at(x, yl, c, z_=z_from), device_id_type=MESH
+            )
 
     each = range(len(chunks))
     for i in each:
         loads[i].wait()
         send(i, OWN_SLOT, X_SLOT, x_sem.at[i], x_mate, x_moves)
     x_slot = jnp.where(x_moves, X_SLOT, OWN_SLOT)
+    def z_send(i, condition):
+        send(i, x_slot, Z_SLOT + half, z_sem.at[half, i], z_dest, condition)
+
     for i in each:
         arrive(i, X_SLOT, x_sem.at[i], x_moves)
-        send(i, x_slot, Z_SLOT + half, z_sem.at[half, i], z_dest, z_moves)
-    away = [jnp.logical_and(even, quarter + 4 * h != z) for h in range(2)]
-    z_slot = [jnp.where(quarter + 4 * h == z, x_slot, Z_SLOT + h) for h in range(2)]
-    for i in each:
-        for h in range(2):
-            arrive(i, Z_SLOT + h, z_sem.at[h, i], away[h])
-            got = got_sem.at[i, y_place]
+        if i == 0:
+            pl.when(z_to > z)(lambda: pl.semaphore_wait(z_ready, 1))
+        z_send(i, z_to != z)
+    away = [jnp.logical_and(even, came + 4 * h != z) for h in range(2)]
+    z_slot = [jnp.where(came + 4 * h == z, x_slot, Z_SLOT + h) for h in range(2)]
+    for h, i in [(h, i) for h in range(2) for i in each]:
+        arrive(i, Z_SLOT + h, z_sem.at[h, i], away[h])
+        got = got_sem.at[i, y_place]
+        if chunks[i][0] in ONE_ROW:
+            goes = jnp.logical_and(even, jnp.logical_not(jnp.logical_and(one_stays, special == h)))
+            send(i, z_slot[h], y_place, got, y_dest(h, special), goes)
+        else:
             send(i, z_slot[h], y_place, got, y_dest(h, 1 - yl), even)
             normal = jnp.logical_and(even, special != h)
             send(i, z_slot[h], y_place, got, y_dest(h, yl), normal)
-    own_slot = [jnp.where(stays[u], z_slot[u], own[u]) for u in range(2)]
+    stay_slot = jnp.where(special == 0, z_slot[0], z_slot[1])
+    own_slot = [own[0], jnp.where(stays, stay_slot, own[1])]
+    one = 4 * quarter + yl + 2 * c
+    one_slot = jnp.where(one_stays, stay_slot, one)
+
+    def one_mine(i):
+        got = got_sem.at[i, one]
+        arrive(i, one, got, jnp.logical_not(one_stays))
+        for to in (x_next[1], x_next[-1], y_mate, core_mate):
+            send(i, one_slot, one, got, to)
+
+    def one_theirs(i, dx, row):
+        k = 4 * ((quarter + 4 + dx * sign) % 4) + 2 * c + (1 - yl if row else yl)
+        got = got_sem.at[i, k]
+        arrive(i, k, got)
+        if row == 0:
+            if dx == -1:
+                send(i, k, k, got, x_next[1])
+            send(i, k, k, got, y_mate)
+        send(i, k, k, got, core_mate)
 
     def mine(i):
+        if chunks[i][0] in ONE_ROW:
+            return one_mine(i)
         for u in range(2):
             got = got_sem.at[i, own[u]]
-            arrive(i, own[u], got, jnp.logical_not(stays[u]))
+            arrive(i, own[u], got, None if u == 0 else jnp.logical_not(stays))
             for to in (x_next[1], x_next[-1]):
                 send(i, own_slot[u], own[u], got, to)
-            send(i, own[u], own[u], got, y_mate, hands_on[u])
+            if u == 1:
+                send(i, own[u], own[u], got, y_mate, hands_on)
             send(i, own_slot[u], own[u], got, core_mate)
 
     def theirs(i, dx):
+        if chunks[i][0] in ONE_ROW:
+            return one_theirs(i, dx, 0)
         for u in range(2):
-            k = 4 * ((quarter + 4 + dx * sign) % 4) + 2 * c + u
+            k = 4 * ((quarter + 4 + dx * sign) % 4) + 2 * c + order[u]
             got = got_sem.at[i, k]
             arrive(i, k, got)
             if dx == -1:
                 send(i, k, k, got, x_next[1])
             send(i, k, k, got, core_mate)
 
-    for i in range(len(chunks) + 2):
-        if i < len(chunks):
-            mine(i)
-        if 0 <= i - 1 < len(chunks):
-            theirs(i - 1, -1)
-            theirs(i - 1, 1)
-        if 0 <= i - 2 < len(chunks):
-            theirs(i - 2, 2)
-
-    for u in range(2):
-
-        @pl.when(stays[u])
+    def tile_of(a):
+        place, source, stayed = (one, one_slot, one_stays) if a in ONE_ROW else (own[1], own_slot[1], stays)
+
+        @pl.when(stayed)
         def _():
-            for a in range(3):
-                held[a, own[u]] = held[a, own_slot[u]]
-
-    for load in weight_loads:
-        load.wait()
-    for j in range(width // tile_rows):
-
-        @pl.when(yh == j)
-        def _():
-            row_part[0] = row_all[pl.ds(j * tile_rows, tile_rows)]
-    part = row_part[...]
-    high = part.astype(jnp.bfloat16).astype(jnp.float32)
-    middle = (part - high).astype(jnp.bfloat16).astype(jnp.float32)
-    low = part - high - middle
-    line = lax.broadcasted_iota(jnp.int32, (8, tile_rows), 0)
-    left = jnp.where(line == 0, high, jnp.where(line == 1, middle, jnp.where(line == 2, low, 0.0)))
-    left = left.astype(jnp.bfloat16)
-    factor = float(tile_rows * CHECK_COLS) ** (-0.5)
-    weight = col_all[...].reshape(1, width) * factor
-    lane = lax.broadcasted_iota(jnp.int32, (1, CHECK_COLS), 1)
-    for a in range(3):
+            held[a, place] = held[a, source]
+
+        if a == 0:
+            for load in weight_loads:
+                load.wait()
+            for j in range(width // tile_rows):
+
+                @pl.when(yh == j)
+                def _():
+                    row_part[0] = row_all[pl.ds(j * tile_rows, tile_rows)]
+
+        part = row_part[...]
+        high = part.astype(jnp.bfloat16).astype(jnp.float32)
+        middle = (part - high).astype(jnp.bfloat16).astype(jnp.float32)
+        low = part - high - middle
+        line = lax.broadcasted_iota(jnp.int32, (8, tile_rows), 0)
+        left = jnp.where(line == 1, middle, jnp.where(line == 2, low, 0.0))
+        left = jnp.where(line == 0, high, left).astype(jnp.bfloat16)
+        factor = float(tile_rows * CHECK_COLS) ** (-0.5)
+        weight = col_all[...].reshape(1, width) * factor
+        lane = lax.broadcasted_iota(jnp.int32, (1, CHECK_COLS), 1)
         for k in range(16):
             for i in each:
                 if chunks[i][0] == a:
@@ -212,6 +243,21 @@
             part_sum = jnp.sum(mixed[:, e * CHECK_COLS : (e + 1) * CHECK_COLS], axis=1, keepdims=True)
             sums = jnp.where(lane == e, part_sum, sums)
         check_ref[a, 0] = sums[:, : width // CHECK_COLS]
+
+    last = len(chunks)
+    for i in range(last + 2):
+        if i < last:
+            mine(i)
+        if 0 <= i - 1 < last:
+            theirs(i - 1, -1)
+            theirs(i - 1, 1)
+        if 0 <= i - 2 < last:
+            theirs(i - 2, 2)
+        if 0 <= i - 3 < last and chunks[i - 3][0] in ONE_ROW:
+            for dx in (0, -1, 1, 2):
+                one_theirs(i - 3, dx, 1)
+    for a in range(3):
+        tile_of(a)
 
     for condition, copy in sends:
         if condition is None:
@@ -252,6 +298,7 @@
             pltpu.SemaphoreType.DMA((2, n)),
             pltpu.SemaphoreType.DMA((n, 16)),
             pltpu.SemaphoreType.DMA((n * 24,)),
+            pltpu.SemaphoreType.REGULAR,
         ],
         compiler_params=pltpu.CompilerParams(
             collective_id=0, has_side_effects=True, vmem_limit_bytes=60 * 2**20

time: 52.4 us -> 47.7 us (0.910)
  the two profiles are of different devices: /device:TPU:1 before, /device:TPU:17 now
where the time goes in v3:
time: 47.7 us; the launch traced here: 47.5 us
  Pallas kernels  46.9 us (98%)
  between operations  0.64 us (1%)
    pallas_call x1, Pallas kernels, shards(): pl.pallas_call(kernel, out_shape=(pltpu.VMEM(*tile),) * 3 + (pltpu.VMEM(*...  45.2 us
    pallas_call x1, Pallas kernels, shards(): pl.pallas_call(store, out_shape=(jax.ShapeDtypeStruct(*tile),) * 3 + (jax...  1.64 us

profile of v3, /device:TPU:17, one launch (start us, length us, event | category | flops | bytes accessed | tf_op | source)
XLA Modules:
  0.0 47.5 jit_solution(7937602623842045773)
XLA Ops:
  0.6 45.2 %shard_map.84 = (bf16[352,1408]{1,0:T(8,128)(2,1)S(1)}, bf16[352,1408]{1,0:T(8,128)(2,1)S(1)}, bf16[352,1408]{1,0:T(8,128)(2,1)S(1)}, f32[3,1,1,11]{3,2,1,0:T(1,128)S(1)}) custom-call(bf16[22,1408]{1,0:T(8,128)(2,1)} %w_ref.1, bf16[22,1408]{1,0:T(8,128)(2,1)} %m_ref.1, bf16[22,1408]{1,0:T(8,128)(2,1)} %v_ref.1, f32[1408]{0:T(1024)} %row_ref.1, f32[1408]{0:T(1024)} %col_ref.1), custom_call_target="tpu_custom_call" | custom-call | tf_op jit(solution)/shard_map/pallas_call | solution.py:286
  45.9 1.6 %shard_map.85 = (bf16[352,1408]{1,0:T(8,128)(2,1)}, bf16[352,1408]{1,0:T(8,128)(2,1)}, bf16[352,1408]{1,0:T(8,128)(2,1)}, f32[3,1,1,11]{3,2,1,0:T(1,128)}) custom-call(bf16[352,1408]{1,0:T(8,128)(2,1)S(1)} %get-tuple-element.8.refs_0_, bf16[352,1408]{1,0:T(8,128)(2,1)S(1)} %get-tuple-element.9.refs_1_, bf16[352,1408]{1,0:T(8,128)(2,1)S(1)} %get-tuple-element.10.refs_2_, ...), custom_call_target="tpu_custom_call" | custom-call | tf_op jit(solution)/shard_map/pallas_call | solution.py:307
